TPU v7x, 32 devices: a whole 2x2x4 slice. The times are simulated.
32 devices in a mesh: row: 4 (over y, core), col: 8 (over z, x).
Axes of the slice: x: 2, y: 2, z: 4, core: 2. Of those that a mesh axis runs over, the one named last changes fastest.
Arguments:
- residual: bfloat16 [1024, 8192], P('row', 'col'), may hold values from -6 to 6
- strip_weights: bfloat16 [1024, 512], P('row'), may hold values from -0.375 to 0.375
- bin_weights: bfloat16 [4, 8192, 1024], P('row', 'col'), may hold values from -0.25 to 0.25
- touched: int32 [4, 8, 8], P('row', 'col'), may hold values 0 or 1
- image: float32 [2048, 1024], P('row', 'col'), may hold values from -6 to 6
- precond: float32 [2048, 1024], P('row', 'col'), may hold values from 0.05 to 1.35, as said below
Outputs:
- updated: float32 [2048, 1024], P('row', 'col')
- mean_change: float32 [], replicated
Inputs may be any that keep to these rules, and one draw needn't show every extreme that they name: `precond`: positive.
All inputs are finite; a program needn't handle non-finite values. No bound on the sum of `touched` on one device may be relied on, other than what follows from the above.
Results may differ from a plain program's by a relative error of at most 0.0023.
Values sent between devices are 32-bit elements; how exact they have to be, the bound alone decides.
A program may use at most 64 MiB of HBM per device.

v0:
```python
import jax
import jax.numpy as jnp
from jax import lax
from jax.sharding import PartitionSpec as P

ITERS = 10


tv_weight = 0.25
dual_step = 0.125
radius = 0.25
epsilon = 1e-06


def padded_2(array, sides, width):
    for axis, dim in sides:
        peers, length = (lax.axis_size(axis), array.shape[dim])
        up = [(i, (i + 1) % peers) for i in range(peers - 1)]
        down = [(j, i) for i, j in up]
        last = lax.slice_in_dim(array, length - width, length, axis=dim)
        initial = lax.slice_in_dim(array, 0, width, axis=dim)
        before = lax.ppermute(last, axis, up)
        after = lax.ppermute(initial, axis, down)
        array = jnp.concatenate([before, array, after], axis=dim)
    return array


def passed_along(value, axis, steps):
    count = lax.axis_size(axis)
    initial, last = (max(0, -steps), min(count, count - steps))
    return lax.ppermute(value, axis, [(source, source + steps) for source in range(initial, last)])


def advance(dual, value_band, first_row, first_col, total_rows, total_cols):
    height = dual.shape[1]
    breadth = dual.shape[2]
    potential = (
        dual[0, 1:, 1:]
        - dual[0, :-1, 1:]
        + (dual[1, 1:, 1:] - dual[1, 1:, :-1])
        - value_band[1:, 1:]
    )
    grad_down = potential[1:, :-1] - potential[:-1, :-1]
    grad_right = potential[:-1, 1:] - potential[:-1, :-1]
    row_ids = first_row + 1 + lax.broadcasted_iota(jnp.int32, (height - 2, breadth - 2), 0)
    col_ids = first_col + 1 + lax.broadcasted_iota(jnp.int32, (height - 2, breadth - 2), 1)
    inside = (row_ids >= 0) & (row_ids < total_rows) & (col_ids >= 0) & (col_ids < total_cols)
    grad_down = jnp.where(inside & (row_ids < total_rows - 1), grad_down, 0.0)
    grad_right = jnp.where(inside & (col_ids < total_cols - 1), grad_right, 0.0)
    magnitude = jnp.sqrt(grad_down * grad_down + grad_right * grad_right)
    divisor = 1.0 + dual_step * magnitude
    interior = dual[:, 1:-1, 1:-1]
    return (interior + dual_step * jnp.stack([grad_down, grad_right])) / divisor


def local(residual, strip_weights, bin_weights, touched, image, precond):
    tile_rows = image.shape[0]
    tile_cols = image.shape[1]
    weights_flat = bin_weights[0]
    tile_marks = touched[0, 0].astype(jnp.float32)
    projected = jnp.dot(jnp.transpose(strip_weights), residual, preferred_element_type=jnp.float32)
    high_part = projected.astype(jnp.bfloat16)
    low_part = (projected - high_part.astype(jnp.float32)).astype(jnp.bfloat16)
    chosen = weights_flat
    chosen = chosen.reshape(chosen.shape[0], lax.axis_size("col") * 1, tile_cols)
    product = jnp.einsum("rd,dct->crt", high_part, chosen, preferred_element_type=jnp.float32)
    product = product + jnp.einsum(
        "rd,dct->crt", low_part, chosen, preferred_element_type=jnp.float32
    )
    gradient = lax.psum_scatter(
        product * tile_marks[:, None, None], "col", scatter_dimension=0, tiled=True
    )[0]
    total_rows = tile_rows * lax.axis_size("row")
    total_cols = tile_cols * lax.axis_size("col")
    cell_total = float(total_rows * total_cols)
    step_dir = precond * gradient
    square_sum = lax.psum(jnp.sum(step_dir * step_dir), ("row", "col"))
    spread = jnp.sqrt(square_sum / cell_total + epsilon)
    factor = jnp.minimum(1.0, radius / spread)
    source = image - factor * step_dir
    scaled = source / tv_weight
    row_first = lax.axis_index("row") * tile_rows
    col_first = lax.axis_index("col") * tile_cols
    starting = jnp.zeros((2, tile_rows, tile_cols), jnp.float32)
    scaled_band = padded_2(scaled, (("row", 0), ("col", 1)), 2)

    def deep_turn(turn_index, dual):
        padded = padded_2(dual, (("row", 1), ("col", 2)), 2)
        middle = advance(padded, scaled_band, row_first - 2, col_first - 2, total_rows, total_cols)
        return advance(
            middle, scaled_band[1:-1, 1:-1], row_first - 1, col_first - 1, total_rows, total_cols
        )

    dual = lax.fori_loop(0, ITERS // 2, deep_turn, starting)
    upper = passed_along(dual[0, -1:, :], "row", 1)
    leftward = passed_along(dual[1, :, -1:], "col", 1)
    above = jnp.concatenate([upper, dual[0, :-1, :]], 0)
    beside = jnp.concatenate([leftward, dual[1, :, :-1]], 1)
    divergence = dual[0] - above + (dual[1] - beside)
    updated = source - tv_weight * divergence
    change = updated - image
    mean_change = lax.psum(jnp.sum(change * change), ("row", "col")) / cell_total
    return (updated, mean_change)


def solution(mesh):
    in_specs = (
        P("row", "col"),
        P("row", None),
        P("row", "col", None),
        P("row", "col", None),
        P("row", "col"),
        P("row", "col"),
    )
    out_specs = (P("row", "col"), P())
    return jax.shard_map(local, mesh=mesh, in_specs=in_specs, out_specs=out_specs, check_vma=False)
```

profile of v0, /device:TPU:0, one launch (start us, length us, event | category | flops | bytes accessed | tf_op | source)
XLA Modules:
  0.0 311.0 jit_solution(7566576884387312116)
XLA Ops:
  7.2 2.3 copy.25
  9.6 0.5 fusion.50
  10.0 1.3 fusion.30
  11.3 2.6 multiply_bitcast_fusion
  13.9 71.2 %reduce-scatter.2.cloned.1.call-done = f32[1,512,128]{2,1,0:T(8,128)} async-done(((f32[8,512,128]{2,1,0:T(8,128)}), f32[1,512,128]{2,1,0:T(8,128)}) %reduce-scatter.2.cloned.1.call-update) | async-done | bytes 262160 | tf_op jit(solution)/shard_map/reduce_scatter | solution.py:70
  85.1 1.6 multiply_reduce_fusion.1
  86.8 39.7 %psum.14 = f32[]{:T(128)} all-reduce(f32[]{:T(128)} %multiply_reduce_fusion.1), channel_id=1, replica_groups=mesh['row'=4,'col'=8] {'row','col'}, use_global_device_ids=true, to_apply=%region_2.0 | all-reduce | flops 1 | bytes 8 | tf_op jit(solution)/shard_map/psum | solution.py:77
  127.2 1.0 broadcast_multiply_fusion
  128.2 1.3 collective-permute-start.4
  129.5 1.3 collective-permute-start.5
  130.8 4.4 %collective-permute-done.5 = f32[2,128]{1,0:T(2,128)S(1)} collective-permute-done((f32[2,128]{1,0:T(2,128)S(1)}, f32[2,128]{1,0:T(2,128)S(1)}, u32[]{:S(2)}, u32[]{:S(2)}) %collective-permute-start.5) | collective-permute-done | bytes 1056 | tf_op jit(solution)/shard_map/ppermute | solution.py:23
  135.4 2.5 collective-permute-start.6
  137.9 1.3 collective-permute-start.7
  139.2 9.6 %collective-permute-done.6 = f32[516,2]{1,0:T(8,128)S(1)} collective-permute-done((f32[516,2]{1,0:T(8,128)S(1)}, f32[516,2]{1,0:T(8,128)S(1)}, u32[]{:S(2)}, u32[]{:S(2)}) %collective-permute-start.6) | collective-permute-done | bytes 4160 | tf_op jit(solution)/shard_map/ppermute | solution.py:22
  149.3 91.6 %while.15 = (s32[]{:T(128)}, f32[2,512,128]{1,2,0:T(8,128)S(1)}, s32[]{:T(128)}, s32[]{:T(128)}, f32[516,132]{0,1:T(8,128)S(1)}, /*index=5*/s32[]{:T(128)}, s32[]{:T(128)}, s32[]{:T(128)}, s32[]{:T(128)}) while((s32[]{:T(128)}, f32[2,512,128]{1,2,0:T(8,128)S(1)}, s32[]{:T(128)}, s32[]{:T(128)}, f32[516,132]{0,1:T(8,128)S(1)}, ...), condition=%wide.region_4.5_spmd.clone, body=%wide.region_3.4_spmd.clone.sunk | while | flops 4004691 | bytes 12869747 | solution.py:94
  149.5 1.3 collective-permute-start
  150.8 4.2 %collective-permute-start.1 = (f32[2,2,128]{1,2,0:T(8,128)S(1)}, f32[2,2,128]{1,2,0:T(8,128)S(1)}, u32[]{:S(2)}, u32[]{:S(2)}) collective-permute-start(f32[2,2,128]{1,2,0:T(8,128)S(1)} %get-tuple-element.290), channel_id=1, source_target_pairs={{0,8},{8,16},{16,24},{1,9},{9,17},{17,25},{2,10},{10,18},{18,26},{... | collective-permute-start | bytes 6152 | tf_op jit(solution)/shard_map/while/body/eval_jaxpr/ppermute | solution.py:22
  155.1 0.9 collective-permute-done.1
  156.0 1.3 collective-permute-start.2
  157.3 4.7 %collective-permute-start.3 = (f32[2,516,2]{1,2,0:T(2,128)S(1)}, f32[2,516,2]{1,2,0:T(2,128)S(1)}, u32[]{:S(2)}, u32[]{:S(2)}) collective-permute-start(f32[2,516,2]{1,2,0:T(2,128)S(1)} %get-tuple-element.292), channel_id=1, source_target_pairs={{0,1},{1,2},{2,3},{3,4},{4,5},{5,6},{6,7},{8,9},{9,10},{10,11},{11... | collective-permute-start | bytes 24776 | tf_op jit(solution)/shard_map/while/body/eval_jaxpr/ppermute | solution.py:22
  162.1 1.3 collective-permute-done.3
  163.7 0.4 fusion.65
  164.2 0.3 multiply_add_fusion.4
  164.8 0.5 fusion.70
  166.0 1.3 collective-permute-start
  167.3 4.4 %collective-permute-start.1 = (f32[2,2,128]{1,2,0:T(8,128)S(1)}, f32[2,2,128]{1,2,0:T(8,128)S(1)}, u32[]{:S(2)}, u32[]{:S(2)}) collective-permute-start(f32[2,2,128]{1,2,0:T(8,128)S(1)} %get-tuple-element.290), channel_id=1, source_target_pairs={{0,8},{8,16},{16,24},{1,9},{9,17},{17,25},{2,10},{10,18},{18,26},{... | collective-permute-start | bytes 6152 | tf_op jit(solution)/shard_map/while/body/eval_jaxpr/ppermute | solution.py:22
  171.7 0.9 collective-permute-done.1
  172.7 1.3 collective-permute-start.2
  174.0 5.2 %collective-permute-start.3 = (f32[2,516,2]{1,2,0:T(2,128)S(1)}, f32[2,516,2]{1,2,0:T(2,128)S(1)}, u32[]{:S(2)}, u32[]{:S(2)}) collective-permute-start(f32[2,516,2]{1,2,0:T(2,128)S(1)} %get-tuple-element.292), channel_id=1, source_target_pairs={{0,1},{1,2},{2,3},{3,4},{4,5},{5,6},{6,7},{8,9},{9,10},{10,11},{11... | collective-permute-start | bytes 24776 | tf_op jit(solution)/shard_map/while/body/eval_jaxpr/ppermute | solution.py:22
  179.2 1.3 collective-permute-done.3
  180.8 0.4 fusion.65
  181.3 0.3 multiply_add_fusion.4
  181.9 0.5 fusion.70
  183.1 1.3 collective-permute-start
  184.4 6.2 %collective-permute-start.1 = (f32[2,2,128]{1,2,0:T(8,128)S(1)}, f32[2,2,128]{1,2,0:T(8,128)S(1)}, u32[]{:S(2)}, u32[]{:S(2)}) collective-permute-start(f32[2,2,128]{1,2,0:T(8,128)S(1)} %get-tuple-element.290), channel_id=1, source_target_pairs={{0,8},{8,16},{16,24},{1,9},{9,17},{17,25},{2,10},{10,18},{18,26},{... | collective-permute-start | bytes 6152 | tf_op jit(solution)/shard_map/while/body/eval_jaxpr/ppermute | solution.py:22
  190.7 0.9 collective-permute-done.1
  191.7 1.3 collective-permute-start.2
  193.0 5.7 %collective-permute-start.3 = (f32[2,516,2]{1,2,0:T(2,128)S(1)}, f32[2,516,2]{1,2,0:T(2,128)S(1)}, u32[]{:S(2)}, u32[]{:S(2)}) collective-permute-start(f32[2,516,2]{1,2,0:T(2,128)S(1)} %get-tuple-element.292), channel_id=1, source_target_pairs={{0,1},{1,2},{2,3},{3,4},{4,5},{5,6},{6,7},{8,9},{9,10},{10,11},{11... | collective-permute-start | bytes 24776 | tf_op jit(solution)/shard_map/while/body/eval_jaxpr/ppermute | solution.py:22
  198.7 1.3 collective-permute-done.3
  200.4 0.4 fusion.65
  200.8 0.3 multiply_add_fusion.4
  201.5 0.5 fusion.70
  202.6 1.3 collective-permute-start
  203.9 5.9 %collective-permute-start.1 = (f32[2,2,128]{1,2,0:T(8,128)S(1)}, f32[2,2,128]{1,2,0:T(8,128)S(1)}, u32[]{:S(2)}, u32[]{:S(2)}) collective-permute-start(f32[2,2,128]{1,2,0:T(8,128)S(1)} %get-tuple-element.290), channel_id=1, source_target_pairs={{0,8},{8,16},{16,24},{1,9},{9,17},{17,25},{2,10},{10,18},{18,26},{... | collective-permute-start | bytes 6152 | tf_op jit(solution)/shard_map/while/body/eval_jaxpr/ppermute | solution.py:22
  209.9 0.9 collective-permute-done.1
  210.9 1.3 collective-permute-start.2
  212.2 5.7 %collective-permute-start.3 = (f32[2,516,2]{1,2,0:T(2,128)S(1)}, f32[2,516,2]{1,2,0:T(2,128)S(1)}, u32[]{:S(2)}, u32[]{:S(2)}) collective-permute-start(f32[2,516,2]{1,2,0:T(2,128)S(1)} %get-tuple-element.292), channel_id=1, source_target_pairs={{0,1},{1,2},{2,3},{3,4},{4,5},{5,6},{6,7},{8,9},{9,10},{10,11},{11... | collective-permute-start | bytes 24776 | tf_op jit(solution)/shard_map/while/body/eval_jaxpr/ppermute | solution.py:22
  218.0 1.3 collective-permute-done.3
  219.6 0.4 fusion.65
  220.1 0.3 multiply_add_fusion.4
  220.7 0.5 fusion.70
  221.8 1.3 collective-permute-start
  223.1 5.9 %collective-permute-start.1 = (f32[2,2,128]{1,2,0:T(8,128)S(1)}, f32[2,2,128]{1,2,0:T(8,128)S(1)}, u32[]{:S(2)}, u32[]{:S(2)}) collective-permute-start(f32[2,2,128]{1,2,0:T(8,128)S(1)} %get-tuple-element.290), channel_id=1, source_target_pairs={{0,8},{8,16},{16,24},{1,9},{9,17},{17,25},{2,10},{10,18},{18,26},{... | collective-permute-start | bytes 6152 | tf_op jit(solution)/shard_map/while/body/eval_jaxpr/ppermute | solution.py:22
  229.2 0.9 collective-permute-done.1
  230.2 1.3 collective-permute-start.2
  231.5 5.7 %collective-permute-start.3 = (f32[2,516,2]{1,2,0:T(2,128)S(1)}, f32[2,516,2]{1,2,0:T(2,128)S(1)}, u32[]{:S(2)}, u32[]{:S(2)}) collective-permute-start(f32[2,516,2]{1,2,0:T(2,128)S(1)} %get-tuple-element.292), channel_id=1, source_target_pairs={{0,1},{1,2},{2,3},{3,4},{4,5},{5,6},{6,7},{8,9},{9,10},{10,11},{11... | collective-permute-start | bytes 24776 | tf_op jit(solution)/shard_map/while/body/eval_jaxpr/ppermute | solution.py:22
  237.2 1.3 collective-permute-done.3
  238.9 0.4 fusion.65
  240.0 0.5 fusion.70
  241.5 4.8 %collective-permute-start.9 = (f32[512,1]{1,0:T(8,128)S(1)}, f32[512,1]{1,0:T(8,128)S(1)}, u32[]{:S(2)}, u32[]{:S(2)}) collective-permute-start(f32[512,1]{1,0:T(8,128)S(1)} %copy.23), channel_id=1, source_target_pairs={{0,1},{1,2},{2,3},{3,4},{4,5},{5,6},{6,7},{8,9},{9,10},{10,11},{11... | collective-permute-start | bytes 6152 | tf_op jit(solution)/shard_map/ppermute | solution.py:31
  246.3 5.3 %collective-permute-start.8 = (f32[1,128]{1,0:T(1,128)S(1)}, f32[1,128]{1,0:T(1,128)S(1)}, u32[]{:S(2)}, u32[]{:S(2)}) collective-permute-start(f32[1,128]{1,0:T(1,128)S(1)} %bitcast.70), channel_id=1, source_target_pairs={{0,8},{8,16},{16,24},{1,9},{9,17},{17,25},{2,10},{10,18},{18,26},{... | collective-permute-start | bytes 1544 | tf_op jit(solution)/shard_map/ppermute | solution.py:31
  251.7 0.8 collective-permute-done.8
  252.5 1.5 multiply_reduce_fusion
  253.9 48.4 %psum.15 = f32[]{:T(128)} all-reduce(f32[]{:T(128)} %get-tuple-element.202), channel_id=1, replica_groups=mesh['row'=4,'col'=8] {'row','col'}, use_global_device_ids=true, to_apply=%region_6.7 | all-reduce | flops 1 | bytes 8 | tf_op jit(solution)/shard_map/psum | solution.py:102
  (104 shorter events, 8.5 us)
Async XLA Ops:
  7.2 2.4 copy-start
  7.2 77.9 %reduce-scatter.2.cloned.1.call-start = ((), (), s32[]{:S(2)}) async-start(), calls=%async_computation.1 | async-start | bytes 2359296 | tf_op jit(solution)/shard_map/reduce_scatter | solution.py:70
  7.2 2.3 copy-start.4
  7.2 2.3 copy-start.3
  13.9 71.3 %copy-start.1 = (f32[512,128]{1,0:T(8,128)S(1)}, f32[512,128]{1,0:T(8,128)}, u32[]{:S(2)}) copy-start(f32[512,128]{1,0:T(8,128)} %param.13) | copy-start | bytes 786436
  13.9 113.3 %copy-start.2 = (f32[512,128]{1,0:T(8,128)S(1)}, f32[512,128]{1,0:T(8,128)}, u32[]{:S(2)}) copy-start(f32[512,128]{1,0:T(8,128)} %param.12) | copy-start | bytes 786436
  128.2 2.6 collective-permute-start.4
  129.5 5.8 %collective-permute-start.5 = (f32[2,128]{1,0:T(2,128)S(1)}, f32[2,128]{1,0:T(2,128)S(1)}, u32[]{:S(2)}, u32[]{:S(2)}) collective-permute-start(f32[2,128]{1,0:T(2,128)S(1)} %get-tuple-element.227), channel_id=1, source_target_pairs={{8,0},{16,8},{24,16},{9,1},{17,9},{25,17},{10,2},{18,10},{26,18},{... | collective-permute-start | bytes 3080 | tf_op jit(solution)/shard_map/ppermute | solution.py:23
  135.4 13.4 %collective-permute-start.6 = (f32[516,2]{1,0:T(8,128)S(1)}, f32[516,2]{1,0:T(8,128)S(1)}, u32[]{:S(2)}, u32[]{:S(2)}) collective-permute-start(f32[516,2]{1,0:T(8,128)S(1)} %get-tuple-element.224), channel_id=1, source_target_pairs={{0,1},{1,2},{2,3},{3,4},{4,5},{5,6},{6,7},{8,9},{9,10},{10,11},{11... | collective-permute-start | bytes 12392 | tf_op jit(solution)/shard_map/ppermute | solution.py:22
  137.9 11.0 %collective-permute-start.7 = (f32[516,2]{1,0:T(8,128)S(1)}, f32[516,2]{1,0:T(8,128)S(1)}, u32[]{:S(2)}, u32[]{:S(2)}) collective-permute-start(f32[516,2]{1,0:T(8,128)S(1)} %get-tuple-element.225), channel_id=1, source_target_pairs={{1,0},{2,1},{3,2},{4,3},{5,4},{6,5},{7,6},{9,8},{10,9},{11,10},{12... | collective-permute-start | bytes 12392 | tf_op jit(solution)/shard_map/ppermute | solution.py:23
  149.5 5.6 %collective-permute-start = (f32[2,2,128]{1,2,0:T(8,128)S(1)}, f32[2,2,128]{1,2,0:T(8,128)S(1)}, u32[]{:S(2)}, u32[]{:S(2)}) collective-permute-start(f32[2,2,128]{1,2,0:T(8,128)S(1)} %get-tuple-element.289), channel_id=1, source_target_pairs={{8,0},{16,8},{24,16},{9,1},{17,9},{25,17},{10,2},{18,10},{26,18},{... | collective-permute-start | bytes 6152 | tf_op jit(solution)/shard_map/while/body/eval_jaxpr/ppermute | solution.py:23
  150.8 5.1 %collective-permute-start.1 = (f32[2,2,128]{1,2,0:T(8,128)S(1)}, f32[2,2,128]{1,2,0:T(8,128)S(1)}, u32[]{:S(2)}, u32[]{:S(2)}) collective-permute-start(f32[2,2,128]{1,2,0:T(8,128)S(1)} %get-tuple-element.290), channel_id=1, source_target_pairs={{0,8},{8,16},{16,24},{1,9},{9,17},{17,25},{2,10},{10,18},{18,26},{... | collective-permute-start | bytes 6152 | tf_op jit(solution)/shard_map/while/body/eval_jaxpr/ppermute | solution.py:22
  156.0 6.0 %collective-permute-start.2 = (f32[2,516,2]{1,2,0:T(2,128)S(1)}, f32[2,516,2]{1,2,0:T(2,128)S(1)}, u32[]{:S(2)}, u32[]{:S(2)}) collective-permute-start(f32[2,516,2]{1,2,0:T(2,128)S(1)} %get-tuple-element.291), channel_id=1, source_target_pairs={{1,0},{2,1},{3,2},{4,3},{5,4},{6,5},{7,6},{9,8},{10,9},{11,10},{12... | collective-permute-start | bytes 24776 | tf_op jit(solution)/shard_map/while/body/eval_jaxpr/ppermute | solution.py:23
  157.3 6.1 %collective-permute-start.3 = (f32[2,516,2]{1,2,0:T(2,128)S(1)}, f32[2,516,2]{1,2,0:T(2,128)S(1)}, u32[]{:S(2)}, u32[]{:S(2)}) collective-permute-start(f32[2,516,2]{1,2,0:T(2,128)S(1)} %get-tuple-element.292), channel_id=1, source_target_pairs={{0,1},{1,2},{2,3},{3,4},{4,5},{5,6},{6,7},{8,9},{9,10},{10,11},{11... | collective-permute-start | bytes 24776 | tf_op jit(solution)/shard_map/while/body/eval_jaxpr/ppermute | solution.py:22
  166.0 5.8 %collective-permute-start = (f32[2,2,128]{1,2,0:T(8,128)S(1)}, f32[2,2,128]{1,2,0:T(8,128)S(1)}, u32[]{:S(2)}, u32[]{:S(2)}) collective-permute-start(f32[2,2,128]{1,2,0:T(8,128)S(1)} %get-tuple-element.289), channel_id=1, source_target_pairs={{8,0},{16,8},{24,16},{9,1},{17,9},{25,17},{10,2},{18,10},{26,18},{... | collective-permute-start | bytes 6152 | tf_op jit(solution)/shard_map/while/body/eval_jaxpr/ppermute | solution.py:23
  167.3 5.4 %collective-permute-start.1 = (f32[2,2,128]{1,2,0:T(8,128)S(1)}, f32[2,2,128]{1,2,0:T(8,128)S(1)}, u32[]{:S(2)}, u32[]{:S(2)}) collective-permute-start(f32[2,2,128]{1,2,0:T(8,128)S(1)} %get-tuple-element.290), channel_id=1, source_target_pairs={{0,8},{8,16},{16,24},{1,9},{9,17},{17,25},{2,10},{10,18},{18,26},{... | collective-permute-start | bytes 6152 | tf_op jit(solution)/shard_map/while/body/eval_jaxpr/ppermute | solution.py:22
  172.7 6.5 %collective-permute-start.2 = (f32[2,516,2]{1,2,0:T(2,128)S(1)}, f32[2,516,2]{1,2,0:T(2,128)S(1)}, u32[]{:S(2)}, u32[]{:S(2)}) collective-permute-start(f32[2,516,2]{1,2,0:T(2,128)S(1)} %get-tuple-element.291), channel_id=1, source_target_pairs={{1,0},{2,1},{3,2},{4,3},{5,4},{6,5},{7,6},{9,8},{10,9},{11,10},{12... | collective-permute-start | bytes 24776 | tf_op jit(solution)/shard_map/while/body/eval_jaxpr/ppermute | solution.py:23
  174.0 6.5 %collective-permute-start.3 = (f32[2,516,2]{1,2,0:T(2,128)S(1)}, f32[2,516,2]{1,2,0:T(2,128)S(1)}, u32[]{:S(2)}, u32[]{:S(2)}) collective-permute-start(f32[2,516,2]{1,2,0:T(2,128)S(1)} %get-tuple-element.292), channel_id=1, source_target_pairs={{0,1},{1,2},{2,3},{3,4},{4,5},{5,6},{6,7},{8,9},{9,10},{10,11},{11... | collective-permute-start | bytes 24776 | tf_op jit(solution)/shard_map/while/body/eval_jaxpr/ppermute | solution.py:22
  183.1 7.6 %collective-permute-start = (f32[2,2,128]{1,2,0:T(8,128)S(1)}, f32[2,2,128]{1,2,0:T(8,128)S(1)}, u32[]{:S(2)}, u32[]{:S(2)}) collective-permute-start(f32[2,2,128]{1,2,0:T(8,128)S(1)} %get-tuple-element.289), channel_id=1, source_target_pairs={{8,0},{16,8},{24,16},{9,1},{17,9},{25,17},{10,2},{18,10},{26,18},{... | collective-permute-start | bytes 6152 | tf_op jit(solution)/shard_map/while/body/eval_jaxpr/ppermute | solution.py:23
  184.4 7.2 %collective-permute-start.1 = (f32[2,2,128]{1,2,0:T(8,128)S(1)}, f32[2,2,128]{1,2,0:T(8,128)S(1)}, u32[]{:S(2)}, u32[]{:S(2)}) collective-permute-start(f32[2,2,128]{1,2,0:T(8,128)S(1)} %get-tuple-element.290), channel_id=1, source_target_pairs={{0,8},{8,16},{16,24},{1,9},{9,17},{17,25},{2,10},{10,18},{18,26},{... | collective-permute-start | bytes 6152 | tf_op jit(solution)/shard_map/while/body/eval_jaxpr/ppermute | solution.py:22
  191.7 7.0 %collective-permute-start.2 = (f32[2,516,2]{1,2,0:T(2,128)S(1)}, f32[2,516,2]{1,2,0:T(2,128)S(1)}, u32[]{:S(2)}, u32[]{:S(2)}) collective-permute-start(f32[2,516,2]{1,2,0:T(2,128)S(1)} %get-tuple-element.291), channel_id=1, source_target_pairs={{1,0},{2,1},{3,2},{4,3},{5,4},{6,5},{7,6},{9,8},{10,9},{11,10},{12... | collective-permute-start | bytes 24776 | tf_op jit(solution)/shard_map/while/body/eval_jaxpr/ppermute | solution.py:23
  193.0 7.1 %collective-permute-start.3 = (f32[2,516,2]{1,2,0:T(2,128)S(1)}, f32[2,516,2]{1,2,0:T(2,128)S(1)}, u32[]{:S(2)}, u32[]{:S(2)}) collective-permute-start(f32[2,516,2]{1,2,0:T(2,128)S(1)} %get-tuple-element.292), channel_id=1, source_target_pairs={{0,1},{1,2},{2,3},{3,4},{4,5},{5,6},{6,7},{8,9},{9,10},{10,11},{11... | collective-permute-start | bytes 24776 | tf_op jit(solution)/shard_map/while/body/eval_jaxpr/ppermute | solution.py:22
  202.6 7.3 %collective-permute-start = (f32[2,2,128]{1,2,0:T(8,128)S(1)}, f32[2,2,128]{1,2,0:T(8,128)S(1)}, u32[]{:S(2)}, u32[]{:S(2)}) collective-permute-start(f32[2,2,128]{1,2,0:T(8,128)S(1)} %get-tuple-element.289), channel_id=1, source_target_pairs={{8,0},{16,8},{24,16},{9,1},{17,9},{25,17},{10,2},{18,10},{26,18},{... | collective-permute-start | bytes 6152 | tf_op jit(solution)/shard_map/while/body/eval_jaxpr/ppermute | solution.py:23
  203.9 6.9 %collective-permute-start.1 = (f32[2,2,128]{1,2,0:T(8,128)S(1)}, f32[2,2,128]{1,2,0:T(8,128)S(1)}, u32[]{:S(2)}, u32[]{:S(2)}) collective-permute-start(f32[2,2,128]{1,2,0:T(8,128)S(1)} %get-tuple-element.290), channel_id=1, source_target_pairs={{0,8},{8,16},{16,24},{1,9},{9,17},{17,25},{2,10},{10,18},{18,26},{... | collective-permute-start | bytes 6152 | tf_op jit(solution)/shard_map/while/body/eval_jaxpr/ppermute | solution.py:22
  210.9 7.0 %collective-permute-start.2 = (f32[2,516,2]{1,2,0:T(2,128)S(1)}, f32[2,516,2]{1,2,0:T(2,128)S(1)}, u32[]{:S(2)}, u32[]{:S(2)}) collective-permute-start(f32[2,516,2]{1,2,0:T(2,128)S(1)} %get-tuple-element.291), channel_id=1, source_target_pairs={{1,0},{2,1},{3,2},{4,3},{5,4},{6,5},{7,6},{9,8},{10,9},{11,10},{12... | collective-permute-start | bytes 24776 | tf_op jit(solution)/shard_map/while/body/eval_jaxpr/ppermute | solution.py:23
  212.2 7.1 %collective-permute-start.3 = (f32[2,516,2]{1,2,0:T(2,128)S(1)}, f32[2,516,2]{1,2,0:T(2,128)S(1)}, u32[]{:S(2)}, u32[]{:S(2)}) collective-permute-start(f32[2,516,2]{1,2,0:T(2,128)S(1)} %get-tuple-element.292), channel_id=1, source_target_pairs={{0,1},{1,2},{2,3},{3,4},{4,5},{5,6},{6,7},{8,9},{9,10},{10,11},{11... | collective-permute-start | bytes 24776 | tf_op jit(solution)/shard_map/while/body/eval_jaxpr/ppermute | solution.py:22
  221.8 7.3 %collective-permute-start = (f32[2,2,128]{1,2,0:T(8,128)S(1)}, f32[2,2,128]{1,2,0:T(8,128)S(1)}, u32[]{:S(2)}, u32[]{:S(2)}) collective-permute-start(f32[2,2,128]{1,2,0:T(8,128)S(1)} %get-tuple-element.289), channel_id=1, source_target_pairs={{8,0},{16,8},{24,16},{9,1},{17,9},{25,17},{10,2},{18,10},{26,18},{... | collective-permute-start | bytes 6152 | tf_op jit(solution)/shard_map/while/body/eval_jaxpr/ppermute | solution.py:23
  223.1 6.9 %collective-permute-start.1 = (f32[2,2,128]{1,2,0:T(8,128)S(1)}, f32[2,2,128]{1,2,0:T(8,128)S(1)}, u32[]{:S(2)}, u32[]{:S(2)}) collective-permute-start(f32[2,2,128]{1,2,0:T(8,128)S(1)} %get-tuple-element.290), channel_id=1, source_target_pairs={{0,8},{8,16},{16,24},{1,9},{9,17},{17,25},{2,10},{10,18},{18,26},{... | collective-permute-start | bytes 6152 | tf_op jit(solution)/shard_map/while/body/eval_jaxpr/ppermute | solution.py:22
  230.2 7.0 %collective-permute-start.2 = (f32[2,516,2]{1,2,0:T(2,128)S(1)}, f32[2,516,2]{1,2,0:T(2,128)S(1)}, u32[]{:S(2)}, u32[]{:S(2)}) collective-permute-start(f32[2,516,2]{1,2,0:T(2,128)S(1)} %get-tuple-element.291), channel_id=1, source_target_pairs={{1,0},{2,1},{3,2},{4,3},{5,4},{6,5},{7,6},{9,8},{10,9},{11,10},{12... | collective-permute-start | bytes 24776 | tf_op jit(solution)/shard_map/while/body/eval_jaxpr/ppermute | solution.py:23
  231.5 7.1 %collective-permute-start.3 = (f32[2,516,2]{1,2,0:T(2,128)S(1)}, f32[2,516,2]{1,2,0:T(2,128)S(1)}, u32[]{:S(2)}, u32[]{:S(2)}) collective-permute-start(f32[2,516,2]{1,2,0:T(2,128)S(1)} %get-tuple-element.292), channel_id=1, source_target_pairs={{0,1},{1,2},{2,3},{3,4},{4,5},{5,6},{6,7},{8,9},{9,10},{10,11},{11... | collective-permute-start | bytes 24776 | tf_op jit(solution)/shard_map/while/body/eval_jaxpr/ppermute | solution.py:22
  241.5 11.0 %collective-permute-start.9 = (f32[512,1]{1,0:T(8,128)S(1)}, f32[512,1]{1,0:T(8,128)S(1)}, u32[]{:S(2)}, u32[]{:S(2)}) collective-permute-start(f32[512,1]{1,0:T(8,128)S(1)} %copy.23), channel_id=1, source_target_pairs={{0,1},{1,2},{2,3},{3,4},{4,5},{5,6},{6,7},{8,9},{9,10},{10,11},{11... | collective-permute-start | bytes 6152 | tf_op jit(solution)/shard_map/ppermute | solution.py:31
  246.3 6.1 %collective-permute-start.8 = (f32[1,128]{1,0:T(1,128)S(1)}, f32[1,128]{1,0:T(1,128)S(1)}, u32[]{:S(2)}, u32[]{:S(2)}) collective-permute-start(f32[1,128]{1,0:T(1,128)S(1)} %bitcast.70), channel_id=1, source_target_pairs={{0,8},{8,16},{16,24},{1,9},{9,17},{17,25},{2,10},{10,18},{18,26},{... | collective-permute-start | bytes 1544 | tf_op jit(solution)/shard_map/ppermute | solution.py:31
Sparse Core Ops, SparseCore 0:
  14.0 71.0 reduce-scatter.1
where the time goes:
time: 312 us; the launch traced here: 311 us
  waiting for transfers between devices  97.2 us (31%)
  blocking collectives  88.1 us (28%)
  starting transfers between devices  83.2 us (27%)
  other arithmetic  17 us (5%)
  between operations  16.7 us (5%)
  matrix products  4.29 us (1%)
  local copies, waits for them, and re-layouts  3.66 us (1%)
    reduce_scatter x1, waiting for transfers between devices, local(): lax.psum_scatter(product * tile_marks[:, None, None], 'col', scatter_dime...  71.2 us
    ppermute x12, starting transfers between devices, padded_2(): before = lax.ppermute(last, axis, up)  57.5 us
    psum x1, blocking collectives, local(): lax.psum(jnp.sum(change * change), ('row', 'col')) / cell_total  48.4 us
    psum x1, blocking collectives, local(): square_sum = lax.psum(jnp.sum(step_dir * step_dir), ('row', 'col'))  39.7 us
    ppermute x12, waiting for transfers between devices, padded_2(): before = lax.ppermute(last, axis, up)  20.7 us
    ppermute x12, starting transfers between devices, padded_2(): after = lax.ppermute(initial, axis, down)  15.5 us
    ppermute x2, starting transfers between devices, passed_along(): lax.ppermute(value, axis, [(source, source + steps) for source in range(i...  10.1 us
  transfers between devices with their start and end apart: 27, of which 14 were waited for; matrix products, arithmetic and copies ran while one was open for 0% of the time, Pallas kernels for 0%

commit v1 on v0

v1 whole, which is shorter than its diff:
```python
import functools

import jax
import jax.numpy as jnp
from jax import lax
from jax.experimental import pallas as pl
from jax.experimental.pallas import tpu as pltpu
from jax.sharding import PartitionSpec as P

ITERS = 10
LANES = 128
HALO = 16
PAD = 8
BASE = PAD + HALO

tv_weight = 0.25
dual_step = 0.125
radius = 0.25
epsilon = 1e-06


def kernel(
    n_row, n_col,
    res_ref, strip_ref, bin_ref, touched_ref, image_ref, precond_ref,
    out_ref, mean_ref,
    prod, recv1, send2, recv2,
    img_t, step_t, halo_img, halo_step, strips, prec_t,
    p_ref, q_ref, pot_ref, scaled_ref, mask_d, mask_r,
    sq_row, sq_col, ch_row, ch_col,
    s1, r1, s2, r2,
    img_send, img_recv, step_send, step_recv,
    sq_row_s, sq_row_r, sq_col_s, sq_col_r,
    ch_row_s, ch_row_r, ch_col_s, ch_col_r,
):
    tile_rows, tile_cols = image_ref.shape
    tiles = tile_rows // LANES
    me_r = lax.axis_index("row")
    me_c = lax.axis_index("col")
    groups = n_col // 2
    g = me_c // 2
    b = lax.rem(me_c, 2)
    peer = 2 * g + 1 - b
    total_rows = n_row * tile_rows
    total_cols = n_col * tile_cols
    cell_total = float(total_rows * total_cols)
    main = pl.ds(BASE, tile_cols)

    for ref in (img_t, step_t, halo_img, halo_step, p_ref, q_ref, pot_ref):
        ref[...] = jnp.zeros_like(ref)

    barrier = pltpu.get_barrier_semaphore()
    for d in range(1, n_col):
        pl.semaphore_signal(barrier, inc=1, device_id={"col": lax.rem(me_c + d, n_col)})
    for d in range(1, n_row):
        pl.semaphore_signal(barrier, inc=1, device_id={"row": lax.rem(me_r + d, n_row)})
    pl.semaphore_wait(barrier, n_col - 1 + n_row - 1)

    def remote(src, dst, send, recv, **where):
        return pltpu.make_async_remote_copy(
            src_ref=src, dst_ref=dst, send_sem=send, recv_sem=recv, device_id=where
        )

    up_ok, down_ok = me_r > 0, me_r < n_row - 1
    left_ok, right_ok = me_c > 0, me_c < n_col - 1

    def row_copies(top, bottom, halo, send, recv):
        up = remote(top, halo.at[pl.ds(0, HALO)], send.at[0], recv.at[0], row=jnp.maximum(me_r - 1, 0))
        down = remote(
            bottom, halo.at[pl.ds(LANES - HALO, HALO)], send.at[1], recv.at[1],
            row=jnp.minimum(me_r + 1, n_row - 1),
        )
        return up, down

    def col_copies(field, first, count, at, send, recv):
        span = pl.ds(first, count)
        left = remote(
            field.at[span, pl.ds(BASE, HALO)], field.at[span, pl.ds(BASE + tile_cols, HALO)],
            send.at[at], recv.at[at], col=jnp.maximum(me_c - 1, 0),
        )
        right = remote(
            field.at[span, pl.ds(BASE + tile_cols - HALO, HALO)], field.at[span, pl.ds(PAD, HALO)],
            send.at[at + 1], recv.at[at + 1], col=jnp.minimum(me_c + 1, n_col - 1),
        )
        return left, right

    def start(pair, first_ok, second_ok):
        pl.when(first_ok)(lambda: pair[0].start())
        pl.when(second_ok)(lambda: pair[1].start())

    def wait_recv(pair, first_ok, second_ok):
        pl.when(second_ok)(lambda: pair[0].wait_recv())
        pl.when(first_ok)(lambda: pair[1].wait_recv())

    def wait_send(pair, first_ok, second_ok):
        pl.when(first_ok)(lambda: pair[0].wait_send())
        pl.when(second_ok)(lambda: pair[1].wait_send())

    order = sorted(range(1, groups), key=lambda d: -min(d, groups - d)) + [0]
    firsts = {}
    for d in order:
        to = lax.rem(g + d, groups)
        cols = pl.ds(pl.multiple_of(to * (2 * tile_cols), 2 * tile_cols), 2 * tile_cols)
        product = jnp.dot(res_ref[...], bin_ref[0, :, cols], preferred_element_type=jnp.float32)
        for h in range(2):
            mark = touched_ref[0, 0, 2 * to + h].astype(jnp.float32)
            prod[2 * to + h] = product[:, h * tile_cols:(h + 1) * tile_cols] * mark
        firsts[d] = remote(prod.at[2 * to + 1 - b], recv1.at[to], s1.at[to], r1.at[to], col=peer)
        firsts[d].start()

    img_rows = row_copies(
        image_ref.at[pl.ds(0, HALO)], image_ref.at[pl.ds(tile_rows - HALO, HALO)],
        halo_img, img_send, img_recv,
    )
    start(img_rows, up_ok, down_ok)
    for j in range(tiles):
        rows = pl.ds(j * LANES, LANES)
        img_t[j, main, :] = image_ref[rows, :].T
        prec_t[j] = precond_ref[rows, :].T
    img_cols = col_copies(img_t, 0, tiles, 2, img_send, img_recv)
    start(img_cols, left_ok, right_ok)

    strip_top = strip_ref[:, :LANES].astype(jnp.float32).T[:HALO]
    strip_bottom = strip_ref[:, tile_rows - LANES:].astype(jnp.float32).T[LANES - HALO:]
    strip_edges = jnp.concatenate([strip_top, strip_bottom], 0).astype(jnp.bfloat16)

    depth = img_t.shape[1]
    lane = lax.broadcasted_iota(jnp.int32, (depth, LANES), 1)
    col_ids = me_c * tile_cols - BASE + lax.broadcasted_iota(jnp.int32, (depth, LANES), 0)
    for j in range(tiles + 1):
        if j < tiles:
            row_ids = me_r * tile_rows + j * LANES + lane
        else:
            row_ids = me_r * tile_rows + jnp.where(lane < LANES // 2, tile_rows + lane, lane - LANES)
        inside = (row_ids >= 0) & (row_ids < total_rows) & (col_ids >= 0) & (col_ids < total_cols)
        mask_d[j] = jnp.where(inside & (row_ids < total_rows - 1), dual_step, 0.0)
        mask_r[j] = jnp.where(inside & (col_ids < total_cols - 1), dual_step, 0.0)

    seconds = []
    for d in order:
        to = lax.rem(g + d, groups)
        firsts[d].wait_recv()
        if d:
            send2[to] = prod[2 * to + b] + recv1[to]
            copy = remote(send2.at[to], recv2.at[g], s2.at[to], r2.at[g], col=2 * to + b)
            copy.start()
            seconds.append(copy)

    wait_recv(img_rows, up_ok, down_ok)
    img_t[tiles, main, :] = halo_img[...].T
    img_corner = col_copies(img_t, tiles, 1, 4, img_send, img_recv)
    start(img_corner, left_ok, right_ok)

    sums = prod[2 * g + b] + recv1[g]
    for d in order[:-1]:
        sender = lax.rem(g - d + groups, groups)
        remote(send2.at[sender], recv2.at[sender], s2.at[sender], r2.at[sender], col=peer).wait_recv()
        sums = sums + recv2[sender]

    def parts(x):
        high = x.astype(jnp.bfloat16)
        return high, (x - high.astype(jnp.float32)).astype(jnp.bfloat16)

    high, low = parts(sums)
    edges = jnp.dot(strip_edges, high, preferred_element_type=jnp.float32)
    edges = edges + jnp.dot(strip_edges, low, preferred_element_type=jnp.float32)
    strips[pl.ds(0, HALO), :] = edges[:HALO] * precond_ref[pl.ds(0, HALO), :]
    strips[pl.ds(HALO, HALO), :] = edges[HALO:] * precond_ref[pl.ds(tile_rows - HALO, HALO), :]
    step_rows = row_copies(
        strips.at[pl.ds(0, HALO)], strips.at[pl.ds(HALO, HALO)], halo_step, step_send, step_recv
    )
    start(step_rows, up_ok, down_ok)

    high, low = parts(sums.T)
    square = jnp.zeros((8, LANES), jnp.float32)
    for j in range(tiles):
        weights = strip_ref[:, j * LANES:(j + 1) * LANES]
        grad = jnp.dot(high, weights, preferred_element_type=jnp.float32)
        grad = grad + jnp.dot(low, weights, preferred_element_type=jnp.float32)
        step = prec_t[j] * grad
        step_t[j, main, :] = step
        square = square + jnp.sum((step * step).reshape(tile_cols // 8, 8, LANES), 0)

    def spread_over(value, slots, mine, count, axis, send, recv):
        slots[mine] = value
        copies = []
        for d in range(1, count):
            to = lax.rem(mine + d, count)
            copy = remote(slots.at[mine], slots.at[mine], send.at[to], recv.at[mine], **{axis: to})
            copy.start()
            copies.append(copy)
        return copies

    def collected(slots, mine, count, axis, send, recv):
        for d in range(1, count):
            at = lax.rem(mine + d, count)
            remote(slots.at[at], slots.at[at], send.at[at], recv.at[at], **{axis: at}).wait_recv()
        total = slots[0]
        for i in range(1, count):
            total = total + slots[i]
        return total

    pending = spread_over(square, sq_row, me_r, n_row, "row", sq_row_s, sq_row_r)
    step_cols = col_copies(step_t, 0, tiles, 2, step_send, step_recv)
    start(step_cols, left_ok, right_ok)
    wait_recv(step_rows, up_ok, down_ok)
    step_t[tiles, main, :] = halo_step[...].T
    step_corner = col_copies(step_t, tiles, 1, 4, step_send, step_recv)
    start(step_corner, left_ok, right_ok)
    square = collected(sq_row, me_r, n_row, "row", sq_row_s, sq_row_r)
    pending += spread_over(square, sq_col, me_c, n_col, "col", sq_col_s, sq_col_r)
    for pair in (img_cols, img_corner, step_cols, step_corner):
        wait_recv(pair, left_ok, right_ok)
    square = collected(sq_col, me_c, n_col, "col", sq_col_s, sq_col_r)
    spread = jnp.sqrt(jnp.sum(square, axis=(0, 1), keepdims=True) / cell_total + epsilon)
    factor = jnp.minimum(1.0, radius / spread)
    factor = jnp.broadcast_to(factor, (depth, LANES))
    for j in range(tiles + 1):
        scaled_ref[j] = (img_t[j] - factor * step_t[j]) / tv_weight

    def turned(pieces, shift):
        rolled = [pltpu.roll(piece, shift % LANES, 1) for piece in pieces]
        at = lax.broadcasted_iota(jnp.int32, pieces[0].shape, 1)
        edge = at == (0 if shift > 0 else LANES - 1)
        n = len(pieces)
        return [jnp.where(edge, rolled[(i - shift) % n], rolled[i]) for i in range(n)]

    every = range(tiles + 1)

    def divergence(first, size, count=tiles + 1):
        p = [p_ref[j, pl.ds(first, size), :] for j in every]
        above = turned(p, 1)
        q = [q_ref[j, pl.ds(first, size), :] for j in range(count)]
        beside = [q_ref[j, pl.ds(first - 1, size), :] for j in range(count)]
        return [p[j] - above[j] + (q[j] - beside[j]) for j in range(count)]

    CHUNK = 16

    def turn(low_end, high_end):
        for first in range(low_end, high_end, CHUNK):
            div = divergence(first, CHUNK)
            for j in every:
                pot_ref[j, pl.ds(first, CHUNK), :] = div[j] - scaled_ref[j, pl.ds(first, CHUNK), :]
        for first in range(low_end, high_end, CHUNK):
            here = pl.ds(first, CHUNK)
            pot = [pot_ref[j, here, :] for j in every]
            below = turned(pot, -1)
            for j in every:
                grad_d = (below[j] - pot[j]) * mask_d[j, here, :]
                grad_r = (pot_ref[j, pl.ds(first + 1, CHUNK), :] - pot[j]) * mask_r[j, here, :]
                inverse = 1.0 / (1.0 + jnp.sqrt(grad_d * grad_d + grad_r * grad_r))
                p_ref[j, here, :] = (p_ref[j, here, :] + grad_d) * inverse
                q_ref[j, here, :] = (q_ref[j, here, :] + grad_r) * inverse

    wide = max(0, ITERS - PAD)

    @pl.loop(0, wide)
    def _(_):
        turn(PAD, depth - PAD)

    @pl.loop(wide, ITERS)
    def _(_):
        turn(HALO, depth - HALO)

    moved = jnp.zeros((8, LANES), jnp.float32)
    for first in range(BASE, BASE + tile_cols, CHUNK):
        div = divergence(first, CHUNK, tiles)
        for j in range(tiles):
            here = pl.ds(first, CHUNK)
            updated = tv_weight * (scaled_ref[j, here, :] - div[j])
            pot_ref[j, here, :] = updated
            change = updated - img_t[j, here, :]
            moved = moved + jnp.sum((change * change).reshape(CHUNK // 8, 8, LANES), 0)
    pending += spread_over(moved, ch_row, me_r, n_row, "row", ch_row_s, ch_row_r)
    moved = collected(ch_row, me_r, n_row, "row", ch_row_s, ch_row_r)
    pending += spread_over(moved, ch_col, me_c, n_col, "col", ch_col_s, ch_col_r)
    for j in range(tiles):
        out_ref[pl.ds(j * LANES, LANES), :] = pot_ref[j, main, :].T
    for d in order:
        firsts[d].wait_send()
    for copy in seconds:
        copy.wait_send()
    for pair in (img_rows, step_rows):
        wait_send(pair, up_ok, down_ok)
    for pair in (img_cols, img_corner, step_cols, step_corner):
        wait_send(pair, left_ok, right_ok)
    moved = collected(ch_col, me_c, n_col, "col", ch_col_s, ch_col_r)
    mean_ref[0] = jnp.sum(moved) / cell_total
    for copy in pending:
        copy.wait_send()


def solution(mesh):
    n_row, n_col = mesh.shape["row"], mesh.shape["col"]

    def local(residual, strip_weights, bin_weights, touched, image, precond):
        angles = residual.shape[0]
        tile_rows, tile_cols = image.shape
        tiles = tile_rows // LANES
        depth = tile_cols + 2 * BASE
        groups = n_col // 2
        f32 = jnp.float32
        vmem = pl.BlockSpec(memory_space=pltpu.VMEM)
        smem = pl.BlockSpec(memory_space=pltpu.SMEM)
        dma = pltpu.SemaphoreType.DMA
        field = pltpu.VMEM((tiles + 1, depth, LANES), f32)
        strip = pltpu.VMEM((LANES, tile_cols), f32)
        updated, mean_change = pl.pallas_call(
            functools.partial(kernel, n_row, n_col),
            out_shape=(
                jax.ShapeDtypeStruct(image.shape, f32),
                jax.ShapeDtypeStruct((1,), f32),
            ),
            in_specs=[vmem, vmem, vmem, smem, vmem, vmem],
            out_specs=(vmem, smem),
            scratch_shapes=[
                pltpu.VMEM((n_col, angles, tile_cols), f32),
                pltpu.VMEM((groups, angles, tile_cols), f32),
                pltpu.VMEM((groups, angles, tile_cols), f32),
                pltpu.VMEM((groups, angles, tile_cols), f32),
                field, field, strip, strip,
                pltpu.VMEM((2 * HALO, tile_cols), f32),
                pltpu.VMEM((tiles, tile_cols, LANES), f32),
                field, field, field, field, field, field,
                pltpu.VMEM((n_row, 8, LANES), f32),
                pltpu.VMEM((n_col, 8, LANES), f32),
                pltpu.VMEM((n_row, 8, LANES), f32),
                pltpu.VMEM((n_col, 8, LANES), f32),
                dma((groups,)), dma((groups,)), dma((groups,)), dma((groups,)),
                dma((6,)), dma((6,)), dma((6,)), dma((6,)),
                dma((n_row,)), dma((n_row,)), dma((n_col,)), dma((n_col,)),
                dma((n_row,)), dma((n_row,)), dma((n_col,)), dma((n_col,)),
            ],
            compiler_params=pltpu.CompilerParams(collective_id=0, has_side_effects=True),
            name="tv_step",
        )(residual, strip_weights, bin_weights, touched, image, precond)
        return updated, mean_change.reshape(())

    in_specs = (
        P("row", "col"),
        P("row", None),
        P("row", "col", None),
        P("row", "col", None),
        P("row", "col"),
        P("row", "col"),
    )
    return jax.shard_map(
        local, mesh=mesh, in_specs=in_specs, out_specs=(P("row", "col"), P()), check_vma=False
    )
```

time: 312 us -> 49.8 us (0.16)
  waiting for transfers between devices: 97.2 us -> 0 us
  blocking collectives: 88.1 us -> 0 us
  starting transfers between devices: 83.2 us -> 0 us
  Pallas kernels: 0 us -> 45.5 us
  other arithmetic: 17 us -> 0 us
  between operations: 16.7 us -> 2.4 us
  matrix products: 4.29 us -> 0 us
    psum x2 -> x0, blocking collectives: 88.1 us -> none  [the longest x1 48.4 us: local(): lax.psum(jnp.sum(change * change), ('row', 'col')) / cell_total]
    ppermute x26 -> x0, starting transfers between devices: 83.1 us -> none  [the longest x12 57.5 us: padded_2(): before = lax.ppermute(last, axis, up)]
    reduce_scatter x1 -> x0, waiting for transfers between devices: 71.2 us -> none  [local(): lax.psum_scatter(product * tile_marks[:, None, None], 'col', scatter_dime...]
    pallas_call x0 -> x1, Pallas kernels: none -> 45.5 us  [local(): pl.pallas_call(functools.partial(kernel, n_row, n_col), out_shape=(jax.Sh...]
    ppermute x26 -> x0, waiting for transfers between devices: 26 us -> none  [the longest x12 20.7 us: padded_2(): before = lax.ppermute(last, axis, up)]
    sub x10 -> x0, other arithmetic: 4.49 us -> none  [advance(): dual[0, 1:, 1:] - dual[0, :-1, 1:] + (dual[1, 1:, 1:] - dual[1, 1:, :-1])]
    dot_general x3 -> x0, matrix products: 4.29 us -> none  [the longest x1 2.59 us: local(): jnp.einsum('rd,dct->crt', high_part, chosen, preferred_element_type=jnp.f...]
    div x11 -> x0, other arithmetic: 3.54 us -> none  [the longest x10 2.54 us: advance(): return (interior + dual_step * jnp.stack([grad_down, grad_right])) / divisor]
  transfers between devices with their start and end apart: 27 -> 0, of which waited for: 14 -> 0; matrix products, arithmetic and copies ran while one was open for 0% -> 0% of each run, Pallas kernels for 0% -> 0%
where the time goes in v1:
time: 49.8 us; the launch traced here: 49.6 us
  Pallas kernels  45.5 us (91%)
  between operations  2.4 us (5%)
  local copies, waits for them, and re-layouts  1.67 us (3%)
    pallas_call x1, Pallas kernels, local(): pl.pallas_call(functools.partial(kernel, n_row, n_col), out_shape=(jax.Sh...  45.5 us
    unnamed x1, local copies, waits for them, and re-layouts  1.67 us

profile of v1, /device:TPU:0, one launch (start us, length us, event | category | flops | bytes accessed | tf_op | source)
XLA Modules:
  0.0 49.6 jit_solution(13371373735122733977)
XLA Ops:
  0.6 45.5 %tv_step.1 = (f32[512,128]{1,0:T(8,128)}, f32[1]{0:T(128)}) custom-call(bf16[256,1024]{1,0:T(8,128)(2,1)} %res_ref.1, bf16[256,512]{1,0:T(8,128)(2,1)} %strip_ref.1, bf16[1,1024,1024]{2,1,0:T(8,128)(2,1)} %bin_ref.1, s32[1,1,8]{2,1,0:T(1,128)} %touched_ref.1, f32[512,128]{1,0:T(8,128)} %image_ref.1, f32[512,128]{1,0:T(8,128)} %precond_ref.1), custom_call_target="tpu_custom_call" | custom-call | tf_op jit(solution)/shard_map/tv_step/pallas_call | solution.py:307
  46.2 1.7 %copy.10 = f32[512,128]{1,0:T(8,128)} copy(f32[512,128]{1,0:T(8,128)} %get-tuple-element.8) | data formatting | bytes 524288

commit v2 on v1

--- a/solution.py
+++ b/solution.py
@@ -27,7 +27,7 @@
     img_t, step_t, halo_img, halo_step, strips, prec_t,
     p_ref, q_ref, pot_ref, scaled_ref, mask_d, mask_r,
     sq_row, sq_col, ch_row, ch_col,
-    s1, r1, s2, r2,
+    s1, r1, s2, r2, bins, bins_sem,
     img_send, img_recv, step_send, step_recv,
     sq_row_s, sq_row_r, sq_col_s, sq_col_r,
     ch_row_s, ch_row_r, ch_col_s, ch_col_r,
@@ -45,6 +45,18 @@
     cell_total = float(total_rows * total_cols)
     main = pl.ds(BASE, tile_cols)
 
+    order = [groups // 2] if groups > 1 else []
+    for i in range((groups - 1) // 2, 0, -1):
+        order += [-i, i]
+    order.append(0)
+    mirror = 1 - 2 * lax.rem(g, 2)
+    targets = [lax.rem(g + mirror * d + groups, groups) for d in order]
+    loads = []
+    for k, to in enumerate(targets):
+        cols = pl.ds(pl.multiple_of(to * (2 * tile_cols), 2 * tile_cols), 2 * tile_cols)
+        loads.append(pltpu.make_async_copy(bin_ref.at[0, :, cols], bins.at[k], bins_sem.at[k]))
+        loads[k].start()
+
     for ref in (img_t, step_t, halo_img, halo_step, p_ref, q_ref, pot_ref):
         ref[...] = jnp.zeros_like(ref)
 
@@ -53,7 +65,6 @@
         pl.semaphore_signal(barrier, inc=1, device_id={"col": lax.rem(me_c + d, n_col)})
     for d in range(1, n_row):
         pl.semaphore_signal(barrier, inc=1, device_id={"row": lax.rem(me_r + d, n_row)})
-    pl.semaphore_wait(barrier, n_col - 1 + n_row - 1)
 
     def remote(src, dst, send, recv, **where):
         return pltpu.make_async_remote_copy(
@@ -95,17 +106,23 @@
         pl.when(first_ok)(lambda: pair[0].wait_send())
         pl.when(second_ok)(lambda: pair[1].wait_send())
 
-    order = sorted(range(1, groups), key=lambda d: -min(d, groups - d)) + [0]
-    firsts = {}
-    for d in order:
-        to = lax.rem(g + d, groups)
-        cols = pl.ds(pl.multiple_of(to * (2 * tile_cols), 2 * tile_cols), 2 * tile_cols)
-        product = jnp.dot(res_ref[...], bin_ref[0, :, cols], preferred_element_type=jnp.float32)
+    half = prod.shape[1] // 2
+    firsts = []
+    for k, to in enumerate(targets):
+        loads[k].wait()
+        product = jnp.dot(res_ref[...], bins[k], preferred_element_type=jnp.float32)
         for h in range(2):
             mark = touched_ref[0, 0, 2 * to + h].astype(jnp.float32)
             prod[2 * to + h] = product[:, h * tile_cols:(h + 1) * tile_cols] * mark
-        firsts[d] = remote(prod.at[2 * to + 1 - b], recv1.at[to], s1.at[to], r1.at[to], col=peer)
-        firsts[d].start()
+        if k == 0:
+            pl.semaphore_wait(barrier, n_col - 1 + n_row - 1)
+        for h in range(2):
+            part = pl.ds(h * half, half)
+            copy = remote(
+                prod.at[2 * to + 1 - b, part], recv1.at[to, part], s1.at[to, h], r1.at[to, h], col=peer
+            )
+            copy.start()
+            firsts.append(copy)
 
     img_rows = row_copies(
         image_ref.at[pl.ds(0, HALO)], image_ref.at[pl.ds(tile_rows - HALO, HALO)],
@@ -136,12 +153,14 @@
         mask_r[j] = jnp.where(inside & (col_ids < total_cols - 1), dual_step, 0.0)
 
     seconds = []
-    for d in order:
-        to = lax.rem(g + d, groups)
-        firsts[d].wait_recv()
-        if d:
-            send2[to] = prod[2 * to + b] + recv1[to]
-            copy = remote(send2.at[to], recv2.at[g], s2.at[to], r2.at[g], col=2 * to + b)
+    for k, to in enumerate(targets[:-1]):
+        for h in range(2):
+            part = pl.ds(h * half, half)
+            firsts[2 * k + h].wait_recv()
+            send2[to, part] = prod[2 * to + b, part] + recv1[to, part]
+            copy = remote(
+                send2.at[to, part], recv2.at[g, part], s2.at[to, h], r2.at[g, h], col=2 * to + b
+            )
             copy.start()
             seconds.append(copy)
 
@@ -150,10 +169,16 @@
     img_corner = col_copies(img_t, tiles, 1, 4, img_send, img_recv)
     start(img_corner, left_ok, right_ok)
 
+    for copy in firsts[-2:]:
+        copy.wait_recv()
     sums = prod[2 * g + b] + recv1[g]
-    for d in order[:-1]:
-        sender = lax.rem(g - d + groups, groups)
-        remote(send2.at[sender], recv2.at[sender], s2.at[sender], r2.at[sender], col=peer).wait_recv()
+    for d in range(1, groups):
+        sender = lax.rem(g + d, groups)
+        for h in range(2):
+            part = pl.ds(h * half, half)
+            remote(
+                send2.at[sender, part], recv2.at[sender, part], s2.at[sender, h], r2.at[sender, h], col=peer
+            ).wait_recv()
         sums = sums + recv2[sender]
 
     def parts(x):
@@ -275,9 +300,7 @@
     pending += spread_over(moved, ch_col, me_c, n_col, "col", ch_col_s, ch_col_r)
     for j in range(tiles):
         out_ref[pl.ds(j * LANES, LANES), :] = pot_ref[j, main, :].T
-    for d in order:
-        firsts[d].wait_send()
-    for copy in seconds:
+    for copy in firsts + seconds:
         copy.wait_send()
     for pair in (img_rows, step_rows):
         wait_send(pair, up_ok, down_ok)
@@ -310,7 +333,7 @@
                 jax.ShapeDtypeStruct(image.shape, f32),
                 jax.ShapeDtypeStruct((1,), f32),
             ),
-            in_specs=[vmem, vmem, vmem, smem, vmem, vmem],
+            in_specs=[vmem, vmem, pl.BlockSpec(memory_space=pl.ANY), smem, vmem, vmem],
             out_specs=(vmem, smem),
             scratch_shapes=[
                 pltpu.VMEM((n_col, angles, tile_cols), f32),
@@ -325,7 +348,8 @@
                 pltpu.VMEM((n_col, 8, LANES), f32),
                 pltpu.VMEM((n_row, 8, LANES), f32),
                 pltpu.VMEM((n_col, 8, LANES), f32),
-                dma((groups,)), dma((groups,)), dma((groups,)), dma((groups,)),
+                dma((groups, 2)), dma((groups, 2)), dma((groups, 2)), dma((groups, 2)),
+                pltpu.VMEM((groups, bin_weights.shape[1], 2 * tile_cols), bin_weights.dtype), dma((groups,)),
                 dma((6,)), dma((6,)), dma((6,)), dma((6,)),
                 dma((n_row,)), dma((n_row,)), dma((n_col,)), dma((n_col,)),
                 dma((n_row,)), dma((n_row,)), dma((n_col,)), dma((n_col,)),

time: 49.8 us -> 47 us (0.944)
  Pallas kernels: 45.5 us -> 42.7 us
    pallas_call x1, Pallas kernels: 45.5 us -> 42.7 us  [local(): pl.pallas_call(functools.partial(kernel, n_row, n_col), out_shape=(jax.Sh...]
where the time goes in v2:
time: 47 us; the launch traced here: 46.8 us
  Pallas kernels  42.7 us (91%)
  between operations  2.4 us (5%)
  local copies, waits for them, and re-layouts  1.67 us (4%)
    pallas_call x1, Pallas kernels, local(): pl.pallas_call(functools.partial(kernel, n_row, n_col), out_shape=(jax.Sh...  42.7 us
    unnamed x1, local copies, waits for them, and re-layouts  1.67 us

profile of v2, /device:TPU:0, one launch (start us, length us, event | category | flops | bytes accessed | tf_op | source)
XLA Modules:
  0.0 46.8 jit_solution(69251329139086587)
XLA Ops:
  0.6 42.7 %tv_step.1 = (f32[512,128]{1,0:T(8,128)}, f32[1]{0:T(128)}) custom-call(bf16[256,1024]{1,0:T(8,128)(2,1)} %res_ref.1, bf16[256,512]{1,0:T(8,128)(2,1)} %strip_ref.1, bf16[1,1024,1024]{2,1,0:T(8,128)(2,1)} %bin_ref.1, s32[1,1,8]{2,1,0:T(1,128)} %touched_ref.1, f32[512,128]{1,0:T(8,128)} %image_ref.1, f32[512,128]{1,0:T(8,128)} %precond_ref.1), custom_call_target="tpu_custom_call" | custom-call | tf_op jit(solution)/shard_map/tv_step/pallas_call | solution.py:330
  43.3 1.7 %copy.10 = f32[512,128]{1,0:T(8,128)} copy(f32[512,128]{1,0:T(8,128)} %get-tuple-element.8) | data formatting | bytes 524288
